TPU v7x, 32 devices: a whole 2x2x4 slice. The times are simulated.
32 devices in a mesh: blk: 8 (over z, y), rep: 4 (over x, core).
Axes of the slice: x: 2, y: 2, z: 4, core: 2. Of those that a mesh axis runs over, the one named last changes fastest.
Arguments:
- tokens: bfloat16 [4096, 8192], P(('blk', 'rep')), may hold values from -6 to 6
- gate_weight: bfloat16 [8, 8192], P('blk'), may hold values from -0.0625 to 0.0625
- up_weight: bfloat16 [8, 8192], P('blk'), may hold values from -0.0625 to 0.0625
- down_weight: bfloat16 [8, 8192], P('blk'), may hold values from -2 to 2
Outputs:
- grad_gate: float32 [8, 8192], P('blk')
- grad_up: float32 [8, 8192], P('blk')
- grad_down: float32 [8, 8192], P('blk')
All inputs are finite; a program needn't handle non-finite values.
Results may differ from a plain program's by a relative error of at most 0.0027.
Values may be sent and summed in bfloat16 or wider, within the bound.
A program may use at most 64 MiB of HBM per device.

v0:
```python
import jax
import jax.numpy as jnp
from jax import lax
from jax.sharding import PartitionSpec as P


def per_device(tokens, gate_weight, up_weight, down_weight):
    tok_rows = tokens.shape[0]
    features = tokens.shape[1]
    cycle_size = lax.axis_size("blk")
    group_size = lax.axis_size("rep")
    loss_scale = float(tok_rows * cycle_size * group_size) ** (-0.5)
    right_numbers = (((1,), (1,)), ((), ()))
    left_numbers = (((0,), (0,)), ((), ()))
    gate_piece = lax.all_gather(gate_weight, "blk", axis=0, tiled=True)
    up_piece = lax.all_gather(up_weight, "blk", axis=0, tiled=True)
    down_piece = lax.all_gather(down_weight, "blk", axis=0, tiled=True)
    gate_pre = lax.dot_general(
        tokens, gate_piece, right_numbers, preferred_element_type=jnp.float32
    )
    up_pre = lax.dot_general(tokens, up_piece, right_numbers, preferred_element_type=jnp.float32)
    hidden_piece = (gate_pre * jax.nn.sigmoid(gate_pre) * up_pre).astype(jnp.bfloat16)
    layer_out = jnp.dot(hidden_piece, down_piece, preferred_element_type=jnp.float32)
    gate_all = gate_pre
    up_all = up_pre
    gate_full = gate_piece
    up_full = up_piece
    down_full = down_piece
    carry = (layer_out, gate_all, up_all, hidden_piece, gate_full, up_full, down_full)
    layer_out, gate_pre, up_pre, hidden, gate_full, up_full, down_full = carry
    cotangent = (layer_out * loss_scale).astype(jnp.bfloat16)
    hidden_grad = lax.dot_general(
        cotangent, down_full, right_numbers, preferred_element_type=jnp.float32
    )
    sigmoid_gate = jax.nn.sigmoid(gate_pre)
    active = gate_pre * sigmoid_gate
    gate_grad = (
        hidden_grad * up_pre * (sigmoid_gate * (1.0 + gate_pre * (1.0 - sigmoid_gate)))
    ).astype(jnp.bfloat16)
    up_grad = (hidden_grad * active).astype(jnp.bfloat16)
    gate_term = lax.dot_general(gate_grad, tokens, left_numbers, preferred_element_type=jnp.float32)
    up_term = lax.dot_general(up_grad, tokens, left_numbers, preferred_element_type=jnp.float32)
    down_term = lax.dot_general(hidden, cotangent, left_numbers, preferred_element_type=jnp.float32)
    shares = lax.psum_scatter(
        jnp.concatenate([gate_term, up_term, down_term], axis=1),
        "blk",
        scatter_dimension=0,
        tiled=True,
    )
    totals = lax.psum(shares, "rep")
    return (totals[:, :features], totals[:, features : 2 * features], totals[:, 2 * features :])


def solution(mesh):
    in_specs = (P(("blk", "rep"), None), P("blk", None), P("blk", None), P("blk", None))
    out_specs = (P("blk", None), P("blk", None), P("blk", None))
    return jax.shard_map(
        per_device, mesh=mesh, in_specs=in_specs, out_specs=out_specs, check_vma=False
    )
```

profile of v0, /device:TPU:0, one launch (start us, length us, event | category | flops | bytes accessed | tf_op | source)
XLA Modules:
  0.0 225.2 jit_solution(10801026277273655064)
XLA Ops:
  7.2 0.0 copy-start
  7.2 0.0 all-reduce.6.cloned.1.call-start
  7.2 32.9 %all-gather.2 = bf16[8,1,8192]{2,1,0:T(2,128)(2,1)S(1)} all-gather(bf16[1,1,8192]{2,1,0:T(2,128)(2,1)} %bitcast.25), channel_id=1, replica_groups=mesh['blk'=8,'rep'=4] {'blk'}, dimensions={0}, use_global_device_ids=true | all-gather | bytes 147456 | tf_op jit(solution)/shard_map/all_gather | solution.py:17
  40.1 30.9 %all-gather = bf16[8,1,8192]{2,1,0:T(2,128)(2,1)S(1)} all-gather(bf16[1,1,8192]{2,1,0:T(2,128)(2,1)} %bitcast.26), channel_id=1, replica_groups=mesh['blk'=8,'rep'=4] {'blk'}, dimensions={0}, use_global_device_ids=true | all-gather | bytes 147456 | tf_op jit(solution)/shard_map/all_gather | solution.py:15
  71.1 30.9 %all-gather.1 = bf16[8,1,8192]{2,1,0:T(2,128)(2,1)S(1)} all-gather(bf16[1,1,8192]{2,1,0:T(2,128)(2,1)} %bitcast.27), channel_id=1, replica_groups=mesh['blk'=8,'rep'=4] {'blk'}, dimensions={0}, use_global_device_ids=true | all-gather | bytes 147456 | tf_op jit(solution)/shard_map/all_gather | solution.py:16
  102.0 0.0 copy-done
  102.0 0.7 fusion.7
  102.7 0.7 multiply_convert_fusion.2
  103.4 0.8 fusion
  104.1 0.6 fusion.1
  104.8 0.4 fusion.20
  105.2 0.4 fusion.14
  105.6 0.0 copy-start.1
  105.6 0.4 fusion.13
  106.0 1.0 pad_maximum_fusion
  106.9 0.0 all-reduce.6.cloned.1.call-update
  107.0 0.0 all-reduce.4.cloned.1.call-start
  107.0 0.0 copy-done.1
  107.0 0.6 dynamic-slice
  107.6 75.8 %all-reduce.6.cloned.1.call-done = f32[8,24576]{1,0:T(8,128)} async-done(((f32[8,24576]{1,0:T(8,128)}), f32[8,24576]{1,0:T(8,128)}) %all-reduce.6.cloned.1.call-update) | async-done | bytes 786448
  183.4 2.5 %constant_dynamic-slice_fusion = f32[1,24576]{1,0:T(1,128)} fusion(f32[8,24576]{1,0:T(8,128)} %all-reduce.6.cloned.1.call-done, u32[]{:T(128)} %bitcast.3), kind=kLoop, calls=%fused_computation.22 | loop fusion | bytes 196612
  185.9 0.0 all-reduce.4.cloned.1.call-update
  185.9 31.0 %all-reduce.4.cloned.1.call-done = f32[1,24576]{1,0:T(1,128)} async-done(((f32[1,24576]{1,0:T(1,128)}), f32[1,24576]{1,0:T(1,128)}) %all-reduce.4.cloned.1.call-update) | async-done | bytes 98320 | tf_op jit(solution)/shard_map/psum | solution.py:50
  216.9 1.4 fusion.19
Async XLA Ops:
  7.2 94.9 %copy-start = (bf16[128,8192]{1,0:T(8,128)(2,1)S(1)}, bf16[128,8192]{1,0:T(8,128)(2,1)}, u32[]{:S(2)}) copy-start(bf16[128,8192]{1,0:T(8,128)(2,1)} %param.4) | copy-start | bytes 6291460
  7.2 176.2 %all-reduce.6.cloned.1.call-start = ((), (), s32[]{:S(2)}) async-start(), calls=%async_computation.1 | async-start | bytes 1572864
  105.6 1.4 copy-start.1
  107.0 109.9 %all-reduce.4.cloned.1.call-start = ((), (), s32[]{:S(2)}) async-start(), calls=%async_computation | async-start | bytes 196608 | tf_op jit(solution)/shard_map/psum | solution.py:50
Sparse Core Ops, SparseCore 0:
  107.1 76.2 all-reduce.5
  186.0 30.8 all-reduce.3
where the time goes:
time: 225 us
  waiting for transfers between devices  107 us (48%)
  blocking collectives  94.8 us (42%)
  between operations  14.1 us (6%)
  local copies, waits for them, and re-layouts  4.51 us (2%)
  matrix products  3.94 us (2%)
    unnamed x3, waiting for transfers between devices  75.8 us
    all_gather x1, blocking collectives, per_device(): down_piece = lax.all_gather(down_weight, 'blk', axis=0, tiled=True)  32.9 us
    psum x1, waiting for transfers between devices, per_device(): totals = lax.psum(shares, 'rep')  31 us
    all_gather x1, blocking collectives, per_device(): gate_piece = lax.all_gather(gate_weight, 'blk', axis=0, tiled=True)  30.9 us
    all_gather x1, blocking collectives, per_device(): up_piece = lax.all_gather(up_weight, 'blk', axis=0, tiled=True)  30.9 us
  transfers between devices with their start and end apart: 2, of which 2 were waited for; matrix products, arithmetic and copies ran while one was open for 0% of the time, Pallas kernels for 0%

commit v1 on v0

--- a/solution.py
+++ b/solution.py
@@ -47,7 +47,9 @@
         scatter_dimension=0,
         tiled=True,
     )
-    totals = lax.psum(shares, "rep")
+    totals = shares
+    for hop in (1, 2):
+        totals = totals + lax.ppermute(totals, "rep", [(dev, dev ^ hop) for dev in range(4)])
     return (totals[:, :features], totals[:, features : 2 * features], totals[:, 2 * features :])
 
 

time: 225 us -> 201 us (0.89)
  waiting for transfers between devices: 107 us -> 80.6 us
    psum x1 -> x0, waiting for transfers between devices: 31 us -> none  [per_device(): totals = lax.psum(shares, 'rep')]
    ppermute x0 -> x2, waiting for transfers between devices: none -> 4.67 us  [per_device(): lax.ppermute(totals, 'rep', [(dev, dev ^ hop) for dev in range(4)])]
    unnamed x3 -> x2, waiting for transfers between devices: 75.8 us -> 75.9 us
  transfers between devices with their start and end apart: 2 -> 3, of which waited for: 2 -> 3; matrix products, arithmetic and copies ran while one was open for 0% -> 0% of each run, Pallas kernels for 0% -> 0%
where the time goes in v1:
time: 201 us
  blocking collectives  94.8 us (47%)
  waiting for transfers between devices  80.6 us (40%)
  between operations  14.1 us (7%)
  matrix products  3.94 us (2%)
  local copies, waits for them, and re-layouts  3.09 us (2%)
  other arithmetic  2.95 us (1%)
    unnamed x2, waiting for transfers between devices  75.9 us
    all_gather x1, blocking collectives, per_device(): down_piece = lax.all_gather(down_weight, 'blk', axis=0, tiled=True)  32.9 us
    all_gather x1, blocking collectives, per_device(): gate_piece = lax.all_gather(gate_weight, 'blk', axis=0, tiled=True)  30.9 us
    all_gather x1, blocking collectives, per_device(): up_piece = lax.all_gather(up_weight, 'blk', axis=0, tiled=True)  30.9 us
    ppermute x2, waiting for transfers between devices, per_device(): lax.ppermute(totals, 'rep', [(dev, dev ^ hop) for dev in range(4)])  4.67 us
  transfers between devices with their start and end apart: 3, of which 3 were waited for; matrix products, arithmetic and copies ran while one was open for 0% of the time, Pallas kernels for 0%

profile of v1, /device:TPU:0, one launch (start us, length us, event | category | flops | bytes accessed | tf_op | source)
XLA Modules:
  0.0 201.0 jit_solution(495450403646162340)
XLA Ops:
  7.2 0.0 copy-start
  7.2 0.0 all-reduce.3.cloned.1.call-start
  7.2 32.9 %all-gather.2 = bf16[8,1,8192]{2,1,0:T(2,128)(2,1)S(1)} all-gather(bf16[1,1,8192]{2,1,0:T(2,128)(2,1)} %bitcast.25), channel_id=1, replica_groups=mesh['blk'=8,'rep'=4] {'blk'}, dimensions={0}, use_global_device_ids=true | all-gather | bytes 147456 | tf_op jit(solution)/shard_map/all_gather | solution.py:17
  40.1 30.9 %all-gather = bf16[8,1,8192]{2,1,0:T(2,128)(2,1)S(1)} all-gather(bf16[1,1,8192]{2,1,0:T(2,128)(2,1)} %bitcast.26), channel_id=1, replica_groups=mesh['blk'=8,'rep'=4] {'blk'}, dimensions={0}, use_global_device_ids=true | all-gather | bytes 147456 | tf_op jit(solution)/shard_map/all_gather | solution.py:15
  71.1 30.9 %all-gather.1 = bf16[8,1,8192]{2,1,0:T(2,128)(2,1)S(1)} all-gather(bf16[1,1,8192]{2,1,0:T(2,128)(2,1)} %bitcast.27), channel_id=1, replica_groups=mesh['blk'=8,'rep'=4] {'blk'}, dimensions={0}, use_global_device_ids=true | all-gather | bytes 147456 | tf_op jit(solution)/shard_map/all_gather | solution.py:16
  102.0 0.0 copy-done
  102.0 0.7 fusion.7
  102.7 0.7 multiply_convert_fusion.2
  103.4 0.8 fusion
  104.1 0.6 fusion.1
  104.8 0.4 fusion.20
  105.2 0.4 fusion.14
  105.6 0.0 copy-start.1
  105.6 0.4 fusion.13
  106.0 0.9 pad_maximum_fusion
  106.9 0.0 all-reduce.3.cloned.1.call-update
  107.0 0.0 copy-done.1
  107.0 0.6 dynamic-slice
  107.5 75.9 %all-reduce.3.cloned.1.call-done = f32[8,24576]{1,0:T(8,128)} async-done(((f32[8,24576]{1,0:T(8,128)}), f32[8,24576]{1,0:T(8,128)}) %all-reduce.3.cloned.1.call-update) | async-done | bytes 786448
  183.4 1.8 constant_dynamic-slice_fusion
  185.3 0.1 collective-permute-start
  185.3 1.3 collective-permute-done
  186.6 1.9 fusion.29
  188.5 1.5 collective-permute-start.1
  190.1 3.4 %collective-permute-done.1 = f32[1,24576]{1,0:T(1,128)S(1)} collective-permute-done((f32[1,24576]{1,0:T(1,128)S(1)}, f32[1,24576]{1,0:T(1,128)S(1)}, u32[]{:S(2)}, u32[]{:S(2)}) %collective-permute-start.1) | collective-permute-done | bytes 98336 | tf_op jit(solution)/shard_map/ppermute | solution.py:52
  193.5 0.1 add.18
  193.6 0.6 fusion.19
Async XLA Ops:
  7.2 94.9 %copy-start = (bf16[128,8192]{1,0:T(8,128)(2,1)S(1)}, bf16[128,8192]{1,0:T(8,128)(2,1)}, u32[]{:S(2)}) copy-start(bf16[128,8192]{1,0:T(8,128)(2,1)} %param.4) | copy-start | bytes 6291460
  7.2 176.2 %all-reduce.3.cloned.1.call-start = ((), (), s32[]{:S(2)}) async-start(), calls=%async_computation | async-start | bytes 1572864
  105.6 1.4 copy-start.1
  185.3 1.4 collective-permute-start
  188.5 4.9 %collective-permute-start.1 = (f32[1,24576]{1,0:T(1,128)S(1)}, f32[1,24576]{1,0:T(1,128)S(1)}, u32[]{:S(2)}, u32[]{:S(2)}) collective-permute-start(f32[1,24576]{1,0:T(1,128)S(1)} %fusion.29), channel_id=1, source_target_pairs={{0,2},{1,3},{2,0},{3,1},{4,6},{5,7},{6,4},{7,5},{8,10},{9,11},{10,... | collective-permute-start | bytes 294920 | tf_op jit(solution)/shard_map/ppermute | solution.py:52
Sparse Core Ops, SparseCore 0:
  107.1 76.2 all-reduce.2
